TPU v7x, 32 devices: a whole 2x2x4 slice. The times are simulated.
32 devices in a mesh: chip: 2 (over y), board: 4 (over z), cuts: 4 (over x, core).
Axes of the slice: x: 2, y: 2, z: 4, core: 2. Of those that a mesh axis runs over, the one named last changes fastest.
Arguments:
- features: bfloat16 [32, 2048, 1024], P(('chip', 'board', 'cuts')), may hold values from -6 to 6
- targets: bfloat16 [32, 2048, 256], P(('chip', 'board', 'cuts')), may hold values from -24 to 24
- lower_weight: bfloat16 [32, 1024, 512], P(('chip', 'board', 'cuts')), may hold values from -0.1875 to 0.1875
- head_weight: float32 [32, 512, 256], P(('chip', 'board', 'cuts')), may hold values from -0.25 to 0.25
- batch_rows: int32 [32, 2, 1024], P(('chip', 'board', 'cuts')), may hold values from 0 to 2047
- sample_counts: int32 [32], P(('chip', 'board', 'cuts')), may hold values from 1 to 1000
- cluster_ids: int32 [32], P(('chip', 'board', 'cuts')), may hold values from 0 to 7, as said below
Outputs:
- cluster_step: float32 [32, 512, 256], P(('chip', 'board', 'cuts'))
Inputs may be any that keep to these rules, and one draw needn't show every extreme that they name: `cluster_ids`: every one of the 8 clusters has at least one client.
All inputs are finite; a program needn't handle non-finite values.
Results may differ from a plain program's by a relative error of at most 0.0003.
Values sent between devices are 32-bit elements; how exact they have to be, the bound alone decides.
No kernel may reach another device: no remote copies, remote signals or barrier semaphores. Data moves between devices by JAX's collectives and lax.ppermute only.
A program may use at most 64 MiB of HBM per device.

v0:
```python
import jax
import jax.numpy as jnp
from jax import lax
from jax.sharding import PartitionSpec as P

LR = 0.5


def on_device(features, targets, lower_weight, head_weight, batch_rows, sample_counts, cluster_ids):
    hidden = jnp.tanh(jnp.dot(features[0], lower_weight[0], preferred_element_type=jnp.float32))
    start = head_weight[0]
    weight = start
    count_rows = batch_rows.shape[2]
    for step in range(batch_rows.shape[1]):
        picked = jnp.take(hidden, batch_rows[0, step], axis=0)
        wanted = jnp.take(targets[0], batch_rows[0, step], axis=0).astype(jnp.float32)
        err = jnp.dot(picked, weight, precision=lax.Precision.HIGHEST) - wanted
        grad = jnp.dot(picked.T, err, precision=lax.Precision.HIGHEST) / count_rows
        weight = weight - LR * grad
    delta = weight - start
    cluster = cluster_ids[0]
    number = 8
    chip_count = lax.axis_size("chip")
    rest_count = lax.axis_size(("board", "cuts"))
    every_id, every_count = (
        lax.all_gather(cluster_ids, ("chip", "board", "cuts"), axis=0, tiled=True),
        lax.all_gather(sample_counts, ("chip", "board", "cuts"), axis=0, tiled=True),
    )
    table = (every_id[:, None] == jnp.arange(number, dtype=jnp.int32)[None, :]).astype(jnp.float32)
    weighted = table * every_count.astype(jnp.float32)[:, None]
    counts = jnp.sum(weighted, axis=0)
    scaled = (sample_counts[0].astype(jnp.float32) * delta).reshape(chip_count, rest_count, -1)
    columns = lax.all_to_all(
        lax.all_to_all(scaled, "chip", split_axis=0, concat_axis=0, tiled=True),
        ("board", "cuts"),
        split_axis=1,
        concat_axis=1,
        tiled=True,
    )
    columns = columns.reshape(chip_count * rest_count, -1)
    share = jnp.dot(table.T, columns, precision=lax.Precision.HIGHEST)
    outgoing = jnp.dot(table, share, precision=lax.Precision.HIGHEST)
    outgoing = outgoing.reshape(chip_count, rest_count, -1)
    arrived = lax.all_to_all(
        lax.all_to_all(outgoing, "chip", split_axis=0, concat_axis=0, tiled=True),
        ("board", "cuts"),
        split_axis=1,
        concat_axis=1,
        tiled=True,
    )
    mine = arrived.reshape(delta.shape)
    denom = lax.dynamic_index_in_dim(counts, cluster, 0, keepdims=False)
    return (mine / (LR * denom))[None]


def solution(mesh):
    return jax.shard_map(
        on_device,
        mesh=mesh,
        in_specs=(
            P(("chip", "board", "cuts"), None, None),
            P(("chip", "board", "cuts"), None, None),
            P(("chip", "board", "cuts"), None, None),
            P(("chip", "board", "cuts"), None, None),
            P(("chip", "board", "cuts"), None, None),
            P(("chip", "board", "cuts")),
            P(("chip", "board", "cuts")),
        ),
        out_specs=P(("chip", "board", "cuts"), None, None),
        check_vma=False,
    )
```

profile of v0, /device:TPU:0, one launch (start us, length us, event | category | flops | bytes accessed | tf_op | source)
XLA Modules:
  0.0 138.6 jit_solution(8541357281149164295)
XLA Ops:
  0.0 0.8 fusion.57
  0.8 0.4 copy-done
  1.3 6.5 %fusion.2 = f32[2048,512]{1,0:T(8,128)} fusion(bf16[1,2048,1024]{2,1,0:T(8,128)(2,1)} %param.11, bf16[1,1024,512]{2,1,0:T(8,128)(2,1)S(1)} %copy-done), kind=kOutput, calls=%fused_computation.6 | convolution fusion | flops 2147483648 | bytes 9437184 | tf_op jit(solution)/shard_map/dot_general | solution.py:10
  7.7 7.5 %gather_fusion = f32[1024,512]{1,0:T(8,128)} fusion(f32[2048,512]{1,0:T(8,128)} %fusion.2, s32[1024]{0:T(1024)S(1)} %fusion.49), kind=kCustom, calls=%fused_computation.clone | custom fusion | bytes 4198400 | tf_op jit(solution)/shard_map/jit(_take)/gather | solution.py:15
  15.3 5.0 %gather_fusion.1 = bf16[1024,256]{1,0:T(8,128)(2,1)} fusion(bf16[2048,256]{1,0:T(8,128)(2,1)S(1)} %bitcast.29, s32[1024]{0:T(1024)S(1)} %fusion.49), kind=kCustom, calls=%fused_computation.1.clone | custom fusion | bytes 1052672 | tf_op jit(solution)/shard_map/jit(_take)/gather | solution.py:16
  20.2 7.5 %gather_fusion.2 = f32[1024,512]{1,0:T(8,128)} fusion(f32[2048,512]{1,0:T(8,128)} %fusion.2, s32[1024]{0:T(1024)S(1)} %fusion.50), kind=kCustom, calls=%fused_computation.2.clone | custom fusion | bytes 4198400 | tf_op jit(solution)/shard_map/jit(_take)/gather | solution.py:15
  27.7 3.9 %gather_fusion.3 = bf16[1024,256]{1,0:T(8,128)(2,1)S(1)} fusion(bf16[2048,256]{1,0:T(8,128)(2,1)S(1)} %bitcast.30, s32[1024]{0:T(1024)S(1)} %fusion.50), kind=kCustom, calls=%fused_computation.3.clone | custom fusion | bytes 1052672 | tf_op jit(solution)/shard_map/jit(_take)/gather | solution.py:16
  31.7 3.7 %fusion.13 = f32[1024,256]{1,0:T(8,128)S(1)} fusion(f32[1024,512]{1,0:T(8,128)} %gather_fusion, pred[1024]{0:T(1024)(128)(4,1)S(1)} %compare_and_fusion.1, f32[1,512,256]{2,1,0:T(8,128)S(1)} %copy-done.4, bf16[1024,256]{1,0:T(8,128)(2,1)} %gather_fusion.1), kind=kOutput, calls=%fused_computation.15 | convolution fusion | flops 1611923456 | bytes 4195328 | tf_op jit(solution)/shard_map/dot_general | solution.py:17
  35.4 3.6 %fusion.34 = f32[512,256]{1,0:T(8,128)S(1)} fusion(f32[1024,256]{1,0:T(8,128)S(1)} %fusion.13, f32[1024,512]{1,0:T(8,128)S(1)} %copy-done.2, pred[1024]{0:T(1024)(128)(4,1)S(1)} %compare_and_fusion.1, f32[1,512,256]{2,1,0:T(8,128)S(1)} %copy-done.4), kind=kOutput, calls=%fused_computation.22 | convolution fusion | flops 1611399168 | bytes 4195328 | tf_op jit(solution)/shard_map/dot_general | solution.py:18
  39.7 2.4 %fusion.16 = f32[1024,256]{1,0:T(8,128)S(1)} fusion(f32[512,256]{1,0:T(8,128)S(1)} %fusion.34, f32[1024,512]{1,0:T(8,128)S(1)} %copy-done.3, pred[1024]{0:T(1024)(128)(4,1)S(1)} %compare_and_fusion, bf16[1024,256]{1,0:T(8,128)(2,1)S(1)} %gather_fusion.3), kind=kOutput, calls=%fused_computation.16 | convolution fusion | flops 1611923456 | bytes 4195328 | tf_op jit(solution)/shard_map/dot_general | solution.py:17
  42.1 3.6 %fusion.31 = f32[512,256]{1,0:T(8,128)S(1)} fusion(f32[512,256]{1,0:T(8,128)S(1)} %fusion.34, f32[1024,256]{1,0:T(8,128)S(1)} %fusion.16, f32[1024,512]{1,0:T(8,128)S(1)} %copy-done.3, pred[1024]{0:T(1024)(128)(4,1)S(1)} %compare_and_fusion, f32[1,512,256]{2,1,0:T(8,128)S(1)} %copy-done.4, f32[]{:T(128)} %bitcast), kind=kOutput, calls=%fused_computation.21 | convolution fusion | flops 1611661312 | bytes 4719620 | tf_op jit(solution)/shard_map/dot_general | solution.py:18
  45.9 12.1 %all_to_all.20 = f32[2,16,4096]{2,1,0:T(8,128)S(1)} all-to-all(f32[2,16,4096]{2,1,0:T(8,128)S(1)} %reshape.37), channel_id=1, replica_groups=mesh['chip'=2,'board'=4,'cuts'=4] {'chip'}, dimensions={0} | all-to-all | bytes 1048576 | tf_op jit(solution)/shard_map/all_to_all | solution.py:34
  58.0 1.2 copy.22
  59.2 5.9 %all-to-all-start.1 = ((f32[2,16,4096]{2,0,1:T(2,128)}), f32[2,16,4096]{2,0,1:T(2,128)S(1)}, u32[]{:S(2)}, u32[]{:S(2)}) async-start(f32[2,16,4096]{2,0,1:T(2,128)} %copy.22), calls=%async_computation.1 | async-start | bytes 1048576 | tf_op jit(solution)/shard_map/all_to_all | solution.py:33
  66.0 40.0 %all-reduce.2 = (s32[32]{0:T(128)S(1)}, s32[32]{0:T(128)S(1)}) all-reduce(s32[32]{0:T(128)S(1)} %dynamic-update-slice, s32[32]{0:T(128)S(1)} %dynamic-update-slice.1), channel_id=1, replica_groups=mesh['chip'=2,'board'=4,'cuts'=4] {'chip','board','cuts'}, use_global_device_ids=true, to_apply=%add | all-reduce | flops 64 | bytes 512
  106.0 0.3 copy.23
  106.6 0.4 fusion.47
  107.0 10.5 %all_to_all.21 = f32[2,16,4096]{2,1,0:T(8,128)S(1)} all-to-all(f32[2,16,4096]{2,1,0:T(8,128)S(1)} %bitcast.32), channel_id=1, replica_groups=mesh['chip'=2,'board'=4,'cuts'=4] {'chip'}, dimensions={0} | all-to-all | bytes 1048576 | tf_op jit(solution)/shard_map/all_to_all | solution.py:45
  117.5 1.2 copy.24
  118.7 4.4 %all-to-all-start.3 = ((f32[2,16,4096]{2,0,1:T(2,128)}), f32[2,16,4096]{2,0,1:T(2,128)S(1)}, u32[]{:S(2)}, u32[]{:S(2)}) async-start(f32[2,16,4096]{2,0,1:T(2,128)} %copy.24), calls=%async_computation.3 | async-start | bytes 1048576 | tf_op jit(solution)/shard_map/all_to_all | solution.py:44
  123.3 0.6 dynamic_slice.4
  124.4 13.0 %all-to-all-done.3 = f32[2,16,4096]{2,0,1:T(2,128)S(1)} async-done(((f32[2,16,4096]{2,0,1:T(2,128)}), f32[2,16,4096]{2,0,1:T(2,128)S(1)}, u32[]{:S(2)}, u32[]{:S(2)}) %all-to-all-start.3) | async-done | bytes 524320 | tf_op jit(solution)/shard_map/all_to_all | solution.py:44
  137.4 0.3 copy_divide_fusion
  137.7 0.9 div.20
  (22 shorter events, 0.8 us)
Async XLA Ops:
  0.0 1.3 copy-start
  7.7 7.5 %copy-start.1 = (bf16[1,2048,256]{2,1,0:T(8,128)(2,1)S(1)}, bf16[1,2048,256]{2,1,0:T(8,128)(2,1)}, u32[]{:S(2)}) copy-start(bf16[1,2048,256]{2,1,0:T(8,128)(2,1)} %param.12) | copy-start | bytes 3145732
  27.7 4.0 %copy-start.4 = (f32[1,512,256]{2,1,0:T(8,128)S(1)}, f32[1,512,256]{2,1,0:T(8,128)}, u32[]{:S(2)}) copy-start(f32[1,512,256]{2,1,0:T(8,128)} %param.14) | copy-start | bytes 1572868
  31.7 3.7 %copy-start.2 = (f32[1024,512]{1,0:T(8,128)S(1)}, f32[1024,512]{1,0:T(8,128)}, u32[]{:S(2)}) copy-start(f32[1024,512]{1,0:T(8,128)} %gather_fusion) | copy-start | bytes 6291460
  35.4 4.3 %copy-start.3 = (f32[1024,512]{1,0:T(8,128)S(1)}, f32[1024,512]{1,0:T(8,128)}, u32[]{:S(2)}) copy-start(f32[1024,512]{1,0:T(8,128)} %gather_fusion.2) | copy-start | bytes 6291460
  59.2 46.8 %all-to-all-start.1 = ((f32[2,16,4096]{2,0,1:T(2,128)}), f32[2,16,4096]{2,0,1:T(2,128)S(1)}, u32[]{:S(2)}, u32[]{:S(2)}) async-start(f32[2,16,4096]{2,0,1:T(2,128)} %copy.22), calls=%async_computation.1 | async-start | bytes 1048576 | tf_op jit(solution)/shard_map/all_to_all | solution.py:33
  118.7 18.7 %all-to-all-start.3 = ((f32[2,16,4096]{2,0,1:T(2,128)}), f32[2,16,4096]{2,0,1:T(2,128)S(1)}, u32[]{:S(2)}, u32[]{:S(2)}) async-start(f32[2,16,4096]{2,0,1:T(2,128)} %copy.24), calls=%async_computation.3 | async-start | bytes 1048576 | tf_op jit(solution)/shard_map/all_to_all | solution.py:44
where the time goes:
time: 139 us
  blocking collectives  62.6 us (45%)
  local copies, waits for them, and re-layouts  29.7 us (21%)
  matrix products  20.5 us (15%)
  waiting for transfers between devices  13 us (9%)
  starting transfers between devices  10.4 us (7%)
  between operations  2.04 us (1%)
    unnamed x1, blocking collectives  40 us
    gather x2, local copies, waits for them, and re-layouts, on_device(): picked = jnp.take(hidden, batch_rows[0, step], axis=0)  15 us
    all_to_all x1, waiting for transfers between devices, on_device(): lax.all_to_all(lax.all_to_all(outgoing, 'chip', split_axis=0, concat_axis...  13 us
    all_to_all x1, blocking collectives, on_device(): lax.all_to_all(scaled, 'chip', split_axis=0, concat_axis=0, tiled=True)  12.1 us
    all_to_all x1, blocking collectives, on_device(): lax.all_to_all(outgoing, 'chip', split_axis=0, concat_axis=0, tiled=True)  10.5 us
    gather x2, local copies, waits for them, and re-layouts, on_device(): jnp.take(targets[0], batch_rows[0, step], axis=0).astype(jnp.float32)  8.91 us
    dot_general x2, matrix products, on_device(): grad = jnp.dot(picked.T, err, precision=lax.Precision.HIGHEST) / count_rows  7.26 us
    dot_general x1, matrix products, on_device(): jnp.dot(features[0], lower_weight[0], preferred_element_type=jnp.float32)  6.46 us
  transfers between devices with their start and end apart: 2, of which 1 were waited for; matrix products, arithmetic and copies ran while one was open for 1% of the time, Pallas kernels for 0%

commit v1 on v0

--- a/solution.py
+++ b/solution.py
@@ -41,12 +41,20 @@
     share = jnp.dot(table.T, columns, precision=lax.Precision.HIGHEST)
     outgoing = jnp.dot(table, share, precision=lax.Precision.HIGHEST)
     outgoing = outgoing.reshape(chip_count, rest_count, -1)
-    arrived = lax.all_to_all(
-        lax.all_to_all(outgoing, "chip", split_axis=0, concat_axis=0, tiled=True),
-        ("board", "cuts"),
-        split_axis=1,
-        concat_axis=1,
-        tiled=True,
+    arrived = jnp.concatenate(
+        lax.all_to_all(
+            jnp.stack(
+                jnp.split(
+                    lax.all_to_all(outgoing, "chip", split_axis=0, concat_axis=0, tiled=True),
+                    lax.axis_size(("board", "cuts")),
+                    axis=1,
+                )
+            ),
+            ("board", "cuts"),
+            0,
+            0,
+        ),
+        axis=1,
     )
     mine = arrived.reshape(delta.shape)
     denom = lax.dynamic_index_in_dim(counts, cluster, 0, keepdims=False)

time: 139 us -> 149 us (1.072)
  local copies, waits for them, and re-layouts: 29.7 us -> 39.2 us
    unnamed x14 -> x29, local copies, waits for them, and re-layouts: 0.65 us -> 10.3 us
where the time goes in v1:
time: 149 us; the launch traced here: 148 us
  blocking collectives  62.6 us (42%)
  local copies, waits for them, and re-layouts  39.2 us (26%)
  matrix products  20.6 us (14%)
  waiting for transfers between devices  12.8 us (9%)
  starting transfers between devices  10.4 us (7%)
  between operations  2.19 us (1%)
    unnamed x1, blocking collectives  39.9 us
    gather x2, local copies, waits for them, and re-layouts, on_device(): picked = jnp.take(hidden, batch_rows[0, step], axis=0)  15.1 us
    all_to_all x1, waiting for transfers between devices, on_device(): lax.all_to_all(jnp.stack(jnp.split(lax.all_to_all(outgoing, 'chip', split...  12.8 us
    all_to_all x1, blocking collectives, on_device(): lax.all_to_all(scaled, 'chip', split_axis=0, concat_axis=0, tiled=True)  12.1 us
    all_to_all x1, blocking collectives, on_device(): lax.all_to_all(outgoing, 'chip', split_axis=0, concat_axis=0, tiled=True)  10.5 us
    unnamed x29, local copies, waits for them, and re-layouts  10.3 us
    gather x2, local copies, waits for them, and re-layouts, on_device(): jnp.take(targets[0], batch_rows[0, step], axis=0).astype(jnp.float32)  8.91 us
    dot_general x2, matrix products, on_device(): grad = jnp.dot(picked.T, err, precision=lax.Precision.HIGHEST) / count_rows  7.28 us
  transfers between devices with their start and end apart: 2, of which 1 were waited for; matrix products, arithmetic and copies ran while one was open for 1% of the time, Pallas kernels for 0%

profile of v1, /device:TPU:0, one launch (start us, length us, event | category | flops | bytes accessed | tf_op | source)
XLA Modules:
  0.0 148.3 jit_solution(5060657107381090459)
XLA Ops:
  0.0 0.8 fusion.73
  1.3 6.5 %fusion.2 = f32[2048,512]{1,0:T(8,128)} fusion(bf16[1,2048,1024]{2,1,0:T(8,128)(2,1)} %param.11, bf16[1,1024,512]{2,1,0:T(8,128)(2,1)S(1)} %copy-done), kind=kOutput, calls=%fused_computation.6 | convolution fusion | flops 2147483648 | bytes 9437184 | tf_op jit(solution)/shard_map/dot_general | solution.py:10
  7.7 7.6 %gather_fusion = f32[1024,512]{1,0:T(8,128)} fusion(f32[2048,512]{1,0:T(8,128)} %fusion.2, s32[1024]{0:T(1024)S(1)} %get-tuple-element.11), kind=kCustom, calls=%fused_computation.clone | custom fusion | bytes 4198400 | tf_op jit(solution)/shard_map/jit(_take)/gather | solution.py:15
  15.3 5.0 %gather_fusion.1 = bf16[1024,256]{1,0:T(8,128)(2,1)} fusion(bf16[2048,256]{1,0:T(8,128)(2,1)S(1)} %bitcast.99, s32[1024]{0:T(1024)S(1)} %get-tuple-element.11), kind=kCustom, calls=%fused_computation.1.clone | custom fusion | bytes 1052672 | tf_op jit(solution)/shard_map/jit(_take)/gather | solution.py:16
  20.3 7.5 %gather_fusion.2 = f32[1024,512]{1,0:T(8,128)} fusion(f32[2048,512]{1,0:T(8,128)} %fusion.2, s32[1024]{0:T(1024)S(1)} %get-tuple-element.12), kind=kCustom, calls=%fused_computation.2.clone | custom fusion | bytes 4198400 | tf_op jit(solution)/shard_map/jit(_take)/gather | solution.py:15
  27.8 3.9 %gather_fusion.3 = bf16[1024,256]{1,0:T(8,128)(2,1)S(1)} fusion(bf16[2048,256]{1,0:T(8,128)(2,1)S(1)} %bitcast.100, s32[1024]{0:T(1024)S(1)} %get-tuple-element.12), kind=kCustom, calls=%fused_computation.3.clone | custom fusion | bytes 1052672 | tf_op jit(solution)/shard_map/jit(_take)/gather | solution.py:16
  31.8 3.7 %fusion.13 = f32[1024,256]{1,0:T(8,128)S(1)} fusion(f32[1024,512]{1,0:T(8,128)} %gather_fusion, pred[1024]{0:T(1024)(128)(4,1)S(1)} %compare_and_fusion.1, f32[1,512,256]{2,1,0:T(8,128)S(1)} %copy-done.4, bf16[1024,256]{1,0:T(8,128)(2,1)} %gather_fusion.1), kind=kOutput, calls=%fused_computation.15 | convolution fusion | flops 1611923456 | bytes 4195328 | tf_op jit(solution)/shard_map/dot_general | solution.py:17
  35.5 3.6 %fusion.34 = f32[512,256]{1,0:T(8,128)S(1)} fusion(f32[1024,256]{1,0:T(8,128)S(1)} %fusion.13, f32[1024,512]{1,0:T(8,128)S(1)} %copy-done.2, pred[1024]{0:T(1024)(128)(4,1)S(1)} %compare_and_fusion.1, f32[1,512,256]{2,1,0:T(8,128)S(1)} %copy-done.4), kind=kOutput, calls=%fused_computation.22 | convolution fusion | flops 1611399168 | bytes 4195328 | tf_op jit(solution)/shard_map/dot_general | solution.py:18
  39.8 2.4 %fusion.16 = f32[1024,256]{1,0:T(8,128)S(1)} fusion(f32[512,256]{1,0:T(8,128)S(1)} %fusion.34, f32[1024,512]{1,0:T(8,128)S(1)} %copy-done.3, pred[1024]{0:T(1024)(128)(4,1)S(1)} %compare_and_fusion, bf16[1024,256]{1,0:T(8,128)(2,1)S(1)} %gather_fusion.3), kind=kOutput, calls=%fused_computation.16 | convolution fusion | flops 1611923456 | bytes 4195328 | tf_op jit(solution)/shard_map/dot_general | solution.py:17
  42.2 3.6 %fusion.31 = f32[512,256]{1,0:T(8,128)S(1)} fusion(f32[512,256]{1,0:T(8,128)S(1)} %fusion.34, f32[1024,256]{1,0:T(8,128)S(1)} %fusion.16, f32[1024,512]{1,0:T(8,128)S(1)} %copy-done.3, pred[1024]{0:T(1024)(128)(4,1)S(1)} %compare_and_fusion, f32[1,512,256]{2,1,0:T(8,128)S(1)} %copy-done.4, f32[]{:T(128)} %bitcast), kind=kOutput, calls=%fused_computation.21 | convolution fusion | flops 1611661312 | bytes 4719620 | tf_op jit(solution)/shard_map/dot_general | solution.py:18
  45.9 12.1 %all_to_all.20 = f32[2,16,4096]{2,1,0:T(8,128)S(1)} all-to-all(f32[2,16,4096]{2,1,0:T(8,128)S(1)} %reshape.37), channel_id=1, replica_groups=mesh['chip'=2,'board'=4,'cuts'=4] {'chip'}, dimensions={0} | all-to-all | bytes 1048576 | tf_op jit(solution)/shard_map/all_to_all | solution.py:34
  58.1 1.2 copy.17
  59.3 5.9 %all-to-all-start.1 = ((f32[2,16,4096]{2,0,1:T(2,128)}), f32[2,16,4096]{2,0,1:T(2,128)S(1)}, u32[]{:S(2)}, u32[]{:S(2)}) async-start(f32[2,16,4096]{2,0,1:T(2,128)} %copy.17), calls=%async_computation.1 | async-start | bytes 1048576 | tf_op jit(solution)/shard_map/all_to_all | solution.py:33
  66.1 39.9 %all-reduce.2 = (s32[32]{0:T(128)S(1)}, s32[32]{0:T(128)S(1)}) all-reduce(s32[32]{0:T(128)S(1)} %dynamic-update-slice, s32[32]{0:T(128)S(1)} %dynamic-update-slice.1), channel_id=1, replica_groups=mesh['chip'=2,'board'=4,'cuts'=4] {'chip','board','cuts'}, use_global_device_ids=true, to_apply=%add | all-reduce | flops 64 | bytes 512
  107.1 10.5 %all_to_all.21 = f32[2,16,4096]{2,1,0:T(8,128)S(1)} all-to-all(f32[2,16,4096]{2,1,0:T(8,128)S(1)} %bitcast.102), channel_id=1, replica_groups=mesh['chip'=2,'board'=4,'cuts'=4] {'chip'}, dimensions={0} | all-to-all | bytes 1048576 | tf_op jit(solution)/shard_map/all_to_all | solution.py:48
  118.2 0.6 fusion.61
  118.9 0.6 fusion.60
  119.5 0.6 fusion.59
  120.1 0.6 fusion.58
  121.4 0.6 fusion.56
  127.9 4.4 %all-to-all-start.3 = ((f32[16,2,1,4096]{3,2,1,0:T(1,128)}), f32[16,2,1,4096]{3,2,1,0:T(1,128)S(1)}, u32[]{:S(2)}, u32[]{:S(2)}) async-start(f32[16,2,1,4096]{3,2,1,0:T(1,128)} %fusion.47), calls=%async_computation.3 | async-start | bytes 1048576 | tf_op jit(solution)/shard_map/all_to_all | solution.py:45
  132.4 0.7 dynamic_slice.4
  133.8 12.8 %all-to-all-done.3 = f32[16,2,1,4096]{3,2,1,0:T(1,128)S(1)} async-done(((f32[16,2,1,4096]{3,2,1,0:T(1,128)}), f32[16,2,1,4096]{3,2,1,0:T(1,128)S(1)}, u32[]{:S(2)}, u32[]{:S(2)}) %all-to-all-start.3) | async-done | bytes 524320 | tf_op jit(solution)/shard_map/all_to_all | solution.py:45
  147.4 0.9 div.24
  (37 shorter events, 9.7 us)
Async XLA Ops:
  0.0 1.3 copy-start
  7.7 7.6 %copy-start.1 = (bf16[1,2048,256]{2,1,0:T(8,128)(2,1)S(1)}, bf16[1,2048,256]{2,1,0:T(8,128)(2,1)}, u32[]{:S(2)}) copy-start(bf16[1,2048,256]{2,1,0:T(8,128)(2,1)} %param.12) | copy-start | bytes 3145732
  27.8 4.0 %copy-start.4 = (f32[1,512,256]{2,1,0:T(8,128)S(1)}, f32[1,512,256]{2,1,0:T(8,128)}, u32[]{:S(2)}) copy-start(f32[1,512,256]{2,1,0:T(8,128)} %param.14) | copy-start | bytes 1572868
  31.7 3.7 %copy-start.2 = (f32[1024,512]{1,0:T(8,128)S(1)}, f32[1024,512]{1,0:T(8,128)}, u32[]{:S(2)}) copy-start(f32[1024,512]{1,0:T(8,128)} %gather_fusion) | copy-start | bytes 6291460
  35.4 4.3 %copy-start.3 = (f32[1024,512]{1,0:T(8,128)S(1)}, f32[1024,512]{1,0:T(8,128)}, u32[]{:S(2)}) copy-start(f32[1024,512]{1,0:T(8,128)} %gather_fusion.2) | copy-start | bytes 6291460
  59.3 46.8 %all-to-all-start.1 = ((f32[2,16,4096]{2,0,1:T(2,128)}), f32[2,16,4096]{2,0,1:T(2,128)S(1)}, u32[]{:S(2)}, u32[]{:S(2)}) async-start(f32[2,16,4096]{2,0,1:T(2,128)} %copy.17), calls=%async_computation.1 | async-start | bytes 1048576 | tf_op jit(solution)/shard_map/all_to_all | solution.py:33
  127.9 18.7 %all-to-all-start.3 = ((f32[16,2,1,4096]{3,2,1,0:T(1,128)}), f32[16,2,1,4096]{3,2,1,0:T(1,128)S(1)}, u32[]{:S(2)}, u32[]{:S(2)}) async-start(f32[16,2,1,4096]{3,2,1,0:T(1,128)} %fusion.47), calls=%async_computation.3 | async-start | bytes 1048576 | tf_op jit(solution)/shard_map/all_to_all | solution.py:45
